TPU v7x, 32 devices: a whole 2x2x4 slice. The times are simulated.
32 devices in a mesh: section: 2 (over core), ctx: 8 (over z, x), dp: 2 (over y).
Axes of the slice: x: 2, y: 2, z: 4, core: 2. Of those that a mesh axis runs over, the one named last changes fastest.
Arguments:
- hidden: bfloat16 [4, 2048, 5376], P(('section', 'dp'), 'ctx'), may hold values from -6 to 6
- frozen_query_rows: bfloat16 [4, 2048, 2048], P(('section', 'dp'), 'ctx'), may hold values from -12 to 12
- frozen_key_rows: bfloat16 [4, 2048, 1024], P(('section', 'dp'), 'ctx'), may hold values from -12 to 12
- frozen_value_rows: bfloat16 [4, 2048, 1024], P(('section', 'dp'), 'ctx'), may hold values from -6 to 6
- next_output_gradient: bfloat16 [4, 2048, 2048], P(('section', 'dp'), 'ctx'), may hold values from -0.011962891 to 0.011962891
- document_lengths: int32 [4, 16], P(('section', 'dp')), may hold values from 1 to 512, 2048 in all within a row
- document_adapter: int32 [4, 16], P(('section', 'dp')), may hold values from 0 to 3
- adapter_down_maps: bfloat16 [5376, 2, 4, 16], replicated, may hold values from -0.078125 to 0.078125
- adapter_up_maps: bfloat16 [2, 4, 16, 1024], replicated, may hold values from -1.5 to 1.5
Outputs:
- handed_on: bfloat16 [4, 2048, 2048], P(('section', 'dp'), 'ctx')
- down_map_gradient: float32 [5376, 2, 4, 16], replicated
- up_map_gradient: float32 [2, 4, 16, 1024], replicated
Inputs may be any that keep to these rules, and one draw needn't show every extreme that they name: `document_lengths`: each sequence's 16 lengths sum to 2048, and the longest is exactly 512.
All inputs are finite; a program needn't handle non-finite values.
Results may differ from a plain program's by a relative error of at most 0.016.
Values may be sent and summed in bfloat16 or wider, within the bound.
No kernel may reach another device: no remote copies, remote signals or barrier semaphores. Data moves between devices by JAX's collectives and lax.ppermute only.
A program may use at most 128 MiB of HBM per device.

v0:
```python
from functools import partial
import jax
import jax.numpy as jnp
from jax import lax
from jax.sharding import PartitionSpec as P

HD = 128
WINDOW = 1024
query_scale = 168.0 ** (-0.5)
adapter_scale = 0.5
rope_base = 10000.0
masked_score = -1e30


def passed_along(value, axis, by):
    length = lax.axis_size(axis)
    return lax.ppermute(value, axis, [(i, (i + by) % length) for i in range(length)])


def passed_along_2(value, axis, steps):
    count = lax.axis_size(axis)
    initial, last = (max(0, -steps), min(count, count - steps))
    return lax.ppermute(value, axis, [(source, source + steps) for source in range(initial, last)])


def rotate(vectors, positions, direction):
    head_dim = vectors.shape[-1]
    half_dim = head_dim // 2
    frequency = rope_base ** (-(jnp.arange(half_dim, dtype=jnp.float32) * 2.0) / head_dim)
    angles = positions[:, None] * frequency[None, :]
    cos_part = jnp.cos(angles)[:, None, :]
    sine_part = direction * jnp.sin(angles)[:, None, :]
    front_half = vectors[..., :half_dim]
    back_half = vectors[..., half_dim:]
    return jnp.concatenate(
        [
            front_half * cos_part - back_half * sine_part,
            back_half * cos_part + front_half * sine_part,
        ],
        axis=-1,
    )


def doc_index(sequence_lengths, positions):
    doc_ends = jnp.cumsum(sequence_lengths)
    return jnp.sum((doc_ends[None, :] <= positions[:, None]).astype(jnp.int32), axis=1)


def tenant_rows(sequence_lengths, adapter_bank, positions):
    doc_ids = doc_index(sequence_lengths, positions)
    picked = (
        doc_ids[:, None] == jnp.arange(sequence_lengths.shape[0], dtype=jnp.int32)[None, :]
    ).astype(jnp.int32)
    return (doc_ids, jnp.sum(picked * adapter_bank[None, :], axis=1))


def adapter_token_rows(
    hidden, frozen_key_rows, frozen_value_rows, adapter_down_maps, adapter_up_maps, adapter_choice
):
    token_row_count = hidden.shape[0]
    adapter_choices = adapter_up_maps.shape[1]
    adapter_rank_size = adapter_up_maps.shape[2]
    key_value_width = adapter_up_maps.shape[3]
    adapter_onehot_mask = (
        adapter_choice[:, None] == jnp.arange(adapter_choices, dtype=jnp.int32)[None, :]
    ).astype(jnp.float32)
    low_rank_rows = jnp.dot(
        hidden,
        adapter_down_maps.reshape(
            adapter_down_maps.shape[0], 2 * adapter_choices * adapter_rank_size
        ),
        preferred_element_type=jnp.float32,
    )
    low_rank_rows = low_rank_rows.reshape(token_row_count, 2, adapter_choices, adapter_rank_size)
    low_rank = jnp.sum(low_rank_rows * adapter_onehot_mask[:, None, :, None], axis=2).astype(
        jnp.bfloat16
    )
    adapter_spread = low_rank[:, :, None, :] * adapter_onehot_mask[:, None, :, None].astype(
        jnp.bfloat16
    )
    key_adapter_shift = jnp.dot(
        adapter_spread[:, 0].reshape(token_row_count, adapter_choices * adapter_rank_size),
        adapter_up_maps[0].reshape(adapter_choices * adapter_rank_size, key_value_width),
        preferred_element_type=jnp.float32,
    )
    value_adapter_shift = jnp.dot(
        adapter_spread[:, 1].reshape(token_row_count, adapter_choices * adapter_rank_size),
        adapter_up_maps[1].reshape(adapter_choices * adapter_rank_size, key_value_width),
        preferred_element_type=jnp.float32,
    )
    key_before_rotary = frozen_key_rows.astype(jnp.float32) + adapter_scale * key_adapter_shift
    value_token_rows = (
        frozen_value_rows.astype(jnp.float32) + adapter_scale * value_adapter_shift
    ).astype(jnp.bfloat16)
    return (adapter_onehot_mask, adapter_spread, key_before_rotary, value_token_rows)


def adapter_gradients(
    hidden, adapter_spread, adapter_onehot_mask, key_gradient, value_gradient, adapter_up_maps
):
    token_row_count = hidden.shape[0]
    adapter_choices = adapter_up_maps.shape[1]
    adapter_rank_size = adapter_up_maps.shape[2]
    key_value_width = adapter_up_maps.shape[3]
    up_gradient_parts = []
    down_parts = []
    for adapter_selector, adapter_field_gradient in ((0, key_gradient), (1, value_gradient)):
        flat_adapter_spread = adapter_spread[:, adapter_selector].reshape(
            token_row_count, adapter_choices * adapter_rank_size
        )
        up_gradient_parts.append(
            adapter_scale
            * jnp.dot(
                flat_adapter_spread.T, adapter_field_gradient, preferred_element_type=jnp.float32
            )
        )
        low_rank_gradient = adapter_scale * jnp.dot(
            adapter_field_gradient,
            adapter_up_maps[adapter_selector]
            .reshape(adapter_choices * adapter_rank_size, key_value_width)
            .T,
            preferred_element_type=jnp.float32,
        )
        down_parts.append(
            (
                low_rank_gradient.reshape(token_row_count, adapter_choices, adapter_rank_size)
                * adapter_onehot_mask[:, :, None]
            ).astype(jnp.bfloat16)
        )
    up_map_gradient = jnp.stack(up_gradient_parts).reshape(
        2, adapter_choices, adapter_rank_size, key_value_width
    )
    low_grads = jnp.stack(down_parts, axis=1).reshape(
        token_row_count, 2 * adapter_choices * adapter_rank_size
    )
    down_map_gradient = jnp.dot(hidden.T, low_grads, preferred_element_type=jnp.float32).reshape(
        hidden.shape[1], 2, adapter_choices, adapter_rank_size
    )
    return (down_map_gradient, up_map_gradient)


def masked_scores(query_part, key_part, allowed):
    scores = (
        jnp.einsum("trd,ld->trl", query_part, key_part, preferred_element_type=jnp.float32)
        * query_scale
    )
    return jnp.where(allowed[:, None, :], scores, masked_score)


def group_forward(operands, allowed):
    query_part, key_part, value_part = operands
    scores = masked_scores(query_part, key_part, allowed)
    row_max = jnp.max(scores, axis=2, keepdims=True)
    shifted = jnp.exp(scores - row_max)
    row_total = jnp.sum(shifted, axis=2, keepdims=True)
    weights = (shifted / row_total).astype(jnp.bfloat16)
    output_rows = jnp.einsum(
        "trl,ld->trd", weights, value_part, preferred_element_type=jnp.float32
    ).astype(jnp.bfloat16)
    return (output_rows, (row_max + jnp.log(row_total))[..., 0])


def group_backward(operands, allowed):
    query_part, key_part, value_part, out_part, grad_part, log_total = operands
    scores = masked_scores(query_part, key_part, allowed)
    weights = jnp.exp(scores - log_total[:, :, None])
    weights_low = weights.astype(jnp.bfloat16)
    drift_rows = jnp.sum(grad_part.astype(jnp.float32) * out_part.astype(jnp.float32), axis=2)
    grad_weights = jnp.einsum(
        "trd,ld->trl", grad_part, value_part, preferred_element_type=jnp.float32
    )
    grad_scores = (weights * (grad_weights - drift_rows[:, :, None])).astype(jnp.bfloat16)
    value_step = jnp.einsum(
        "trl,trd->ld", weights_low, grad_part, preferred_element_type=jnp.float32
    )
    key_step = (
        jnp.einsum("trl,trd->ld", grad_scores, query_part, preferred_element_type=jnp.float32)
        * query_scale
    )
    return (key_step, value_step)


def body(
    hidden,
    frozen_query_rows,
    frozen_key_rows,
    frozen_value_rows,
    next_output_gradient,
    document_lengths,
    document_adapter,
    adapter_down_maps,
    adapter_up_maps,
):
    tok_rows = hidden.shape[1]
    query_width = frozen_query_rows.shape[2]
    key_value_width = frozen_key_rows.shape[2]
    kv_heads = key_value_width // HD
    group_size = query_width // key_value_width
    ctx_index = lax.axis_index("ctx")
    reach_devs = min(WINDOW // tok_rows, lax.axis_size("ctx") - 1)
    returned_values = passed_along(next_output_gradient, "section", -1)
    positions = ctx_index * tok_rows + jnp.arange(tok_rows, dtype=jnp.int32)
    doc_ids, adapter_choice = tenant_rows(document_lengths[0], document_adapter[0], positions)
    adapter_onehot_mask, adapter_spread, key_before_rotary, value_token_rows = adapter_token_rows(
        hidden[0],
        frozen_key_rows[0],
        frozen_value_rows[0],
        adapter_down_maps,
        adapter_up_maps,
        adapter_choice,
    )
    pos_float = positions.astype(jnp.float32)
    key_rows = (
        rotate(key_before_rotary.reshape(tok_rows, kv_heads, HD), pos_float, 1.0)
        .astype(jnp.bfloat16)
        .reshape(tok_rows, key_value_width)
    )
    query_rows = rotate(
        frozen_query_rows[0].astype(jnp.float32).reshape(tok_rows, kv_heads * group_size, HD),
        pos_float,
        1.0,
    ).astype(jnp.bfloat16)
    received = []
    moving = (key_rows, value_token_rows)
    for distance in range(reach_devs):
        moving = passed_along_2((moving[0], moving[1]), "ctx", 1)
        received.append(moving)
    far_first = received[::-1]
    key_all = jnp.concatenate([kv_pair[0] for kv_pair in far_first] + [key_rows], axis=0)
    value_all = jnp.concatenate([kv_pair[1] for kv_pair in far_first] + [value_token_rows], axis=0)
    key_pos = (ctx_index - reach_devs) * tok_rows + jnp.arange(
        (reach_devs + 1) * tok_rows, dtype=jnp.int32
    )
    key_docs = doc_index(document_lengths[0], key_pos)
    key_gap = positions[:, None] - key_pos[None, :]
    allowed = (
        (doc_ids[:, None] == key_docs[None, :])
        & (key_gap >= 0)
        & (key_gap < WINDOW)
        & (key_pos >= 0)[None, :]
    )
    query_groups = jnp.moveaxis(query_rows.reshape(tok_rows, kv_heads, group_size, HD), 1, 0)
    key_groups = jnp.moveaxis(key_all.reshape(-1, kv_heads, HD), 1, 0)
    value_groups = jnp.moveaxis(value_all.reshape(-1, kv_heads, HD), 1, 0)
    out_groups, log_groups = lax.map(
        partial(group_forward, allowed=allowed), (query_groups, key_groups, value_groups)
    )
    attention_output = jnp.moveaxis(out_groups, 0, 1).reshape(1, tok_rows, query_width)
    handed = passed_along(attention_output, "section", 1)
    grad_groups = jnp.moveaxis(returned_values[0].reshape(tok_rows, kv_heads, group_size, HD), 1, 0)
    key_grads, value_grads = lax.map(
        partial(group_backward, allowed=allowed),
        (query_groups, key_groups, value_groups, out_groups, grad_groups, log_groups),
    )
    key_grads = jnp.moveaxis(key_grads, 0, 1).reshape(-1, key_value_width)
    value_grads = jnp.moveaxis(value_grads, 0, 1).reshape(-1, key_value_width)

    def rows_at(field_rows, distance):
        return field_rows[
            (reach_devs - distance) * tok_rows : (reach_devs - distance + 1) * tok_rows
        ]

    carried = (rows_at(key_grads, reach_devs), rows_at(value_grads, reach_devs))
    for distance in range(reach_devs - 1, -1, -1):
        carried = passed_along_2((carried[0], carried[1]), "ctx", -1)
        carried = (
            carried[0] + rows_at(key_grads, distance),
            carried[1] + rows_at(value_grads, distance),
        )
    key_back, value_back = carried
    key_gradient = (
        rotate(key_back.reshape(tok_rows, kv_heads, HD), pos_float, -1.0)
        .astype(jnp.bfloat16)
        .reshape(tok_rows, key_value_width)
    )
    value_gradient = value_back.astype(jnp.bfloat16)
    down_map_gradient, up_map_gradient = adapter_gradients(
        hidden[0],
        adapter_spread,
        adapter_onehot_mask,
        key_gradient,
        value_gradient,
        adapter_up_maps,
    )
    summed = lax.psum((down_map_gradient, up_map_gradient), ("section", "ctx", "dp"))
    return (handed, summed[0], summed[1])


def solution(mesh):
    return jax.shard_map(
        body,
        mesh=mesh,
        in_specs=(
            P(("section", "dp"), "ctx", None),
            P(("section", "dp"), "ctx", None),
            P(("section", "dp"), "ctx", None),
            P(("section", "dp"), "ctx", None),
            P(("section", "dp"), "ctx", None),
            P(("section", "dp"), None),
            P(("section", "dp"), None),
            P(),
            P(),
        ),
        out_specs=(P(("section", "dp"), "ctx", None), P(), P()),
        check_vma=False,
    )
```

profile of v0, /device:TPU:0, one launch (start us, length us, event | category | flops | bytes accessed | tf_op | source)
XLA Modules:
  0.0 638.7 jit_solution(13565225289575519029)
XLA Ops:
  9.2 2.4 fusion.65
  13.0 2.5 copy.58
  17.9 5.7 collective-permute-start
  24.7 3.5 collective-permute-start.4
  28.1 6.9 %collective-permute-done = bf16[256,1024]{0,1:T(8,128)(2,1)} collective-permute-done((bf16[256,1024]{0,1:T(8,128)(2,1)S(1)}, bf16[256,1024]{0,1:T(8,128)(2,1)}, u32[]{:S(2)}, u32[]{:S(2)}) %collective-permute-start) | collective-permute-done | bytes 524320 | tf_op jit(solution)/shard_map/ppermute | solution.py:23
  35.0 5.3 collective-permute-start.1
  42.6 2.8 convert_bitcast_fusion
  46.4 5.2 collective-permute-start.5
  51.5 6.1 collective-permute-done.1
  57.6 5.2 collective-permute-start.2
  68.8 5.2 collective-permute-start.6
  74.0 6.0 collective-permute-done.2
  80.1 4.4 collective-permute-start.3
  87.5 3.8 collective-permute-done.6
  91.3 5.2 collective-permute-start.7
  96.5 6.1 collective-permute-done.3
  109.8 4.4 copy.48
  121.6 46.0 %while.26 = (s32[]{:T(128)}, bf16[8,256,2,128]{3,1,2,0:T(8,128)(2,1)}, f32[8,256,2]{1,2,0:T(2,128)}, bf16[8,256,2,128]{3,1,2,0:T(8,128)(2,1)}, bf16[8,1280,128]{...) while((s32[]{:T(128)}, ...), condition=%wide.region_8.9_spmd.clone, body=%wide.region_5.8_spmd.clone.sunk | while | flops 343145984 | bytes 9469813 | solution.py:245
  130.9 2.3 fusion.119
  136.6 2.3 fusion.119
  142.4 2.3 fusion.119
  148.2 2.3 fusion.119
  159.6 2.3 fusion.119
  165.4 2.3 fusion.119
  167.7 127.0 %while.27 = (s32[]{:T(128)}, f32[8,1280,128]{1,2,0:T(8,128)}, f32[8,1280,128]{1,2,0:T(8,128)}, bf16[8,256,2,128]{3,1,2,0:T(8,128)(2,1)}, bf16[8,1280,128]{2,1,0:...) while((s32[]{:T(128)}, f32[8,1280,128]{1,2,0:T(8,128)}, ...), condition=%wide.region_11.12_spmd.clone, body=%wide.region_9.11_spmd.clone.sunk | while | flops 678395392 | bytes 14472769 | solution.py:251
  168.9 3.3 fusion.128
  174.3 3.9 fusion.130
  180.4 3.0 fusion.131
  184.8 3.3 fusion.128
  190.2 3.9 fusion.130
  196.3 3.0 fusion.131
  200.6 3.3 fusion.128
  206.1 3.9 fusion.130
  212.2 3.1 fusion.131
  216.6 3.3 fusion.128
  222.0 3.9 fusion.130
  228.1 3.1 fusion.131
  232.5 3.3 fusion.128
  238.0 3.9 fusion.130
  244.1 3.0 fusion.131
  248.3 3.3 fusion.128
  253.8 3.9 fusion.130
  259.9 3.0 fusion.131
  264.2 3.3 fusion.128
  269.7 3.9 fusion.130
  275.8 3.0 fusion.131
  280.1 3.3 fusion.128
  285.5 3.9 fusion.130
  291.7 3.0 fusion.131
  294.7 3.0 fusion.84
  301.2 24.9 %collective-permute-done.14 = f32[256,1024]{0,1:T(8,128)S(1)} collective-permute-done((f32[256,1024]{0,1:T(8,128)S(1)}, f32[256,1024]{0,1:T(8,128)S(1)}, u32[]{:S(2)}, u32[]{:S(2)}) %collective-permute-start.14) | collective-permute-done | bytes 1048608 | tf_op jit(solution)/shard_map/ppermute | solution.py:23
  327.6 21.0 %collective-permute-done.10 = f32[256,1024]{0,1:T(8,128)S(1)} collective-permute-done((f32[256,1024]{0,1:T(8,128)S(1)}, f32[256,1024]{0,1:T(8,128)S(1)}, u32[]{:S(2)}, u32[]{:S(2)}) %collective-permute-start.10) | collective-permute-done | bytes 1048608 | tf_op jit(solution)/shard_map/ppermute | solution.py:23
  350.1 21.0 %collective-permute-done.15 = f32[256,1024]{0,1:T(8,128)S(1)} collective-permute-done((f32[256,1024]{0,1:T(8,128)S(1)}, f32[256,1024]{0,1:T(8,128)S(1)}, u32[]{:S(2)}, u32[]{:S(2)}) %collective-permute-start.15) | collective-permute-done | bytes 1048608 | tf_op jit(solution)/shard_map/ppermute | solution.py:23
  372.6 21.0 %collective-permute-done.11 = f32[256,1024]{0,1:T(8,128)S(1)} collective-permute-done((f32[256,1024]{0,1:T(8,128)S(1)}, f32[256,1024]{0,1:T(8,128)S(1)}, u32[]{:S(2)}, u32[]{:S(2)}) %collective-permute-start.11) | collective-permute-done | bytes 1048608 | tf_op jit(solution)/shard_map/ppermute | solution.py:23
  395.0 21.0 %collective-permute-done.16 = f32[256,1024]{0,1:T(8,128)S(1)} collective-permute-done((f32[256,1024]{0,1:T(8,128)S(1)}, f32[256,1024]{0,1:T(8,128)S(1)}, u32[]{:S(2)}, u32[]{:S(2)}) %collective-permute-start.16) | collective-permute-done | bytes 1048608 | tf_op jit(solution)/shard_map/ppermute | solution.py:23
  417.5 21.0 %collective-permute-done.12 = f32[256,1024]{0,1:T(8,128)S(1)} collective-permute-done((f32[256,1024]{0,1:T(8,128)S(1)}, f32[256,1024]{0,1:T(8,128)S(1)}, u32[]{:S(2)}, u32[]{:S(2)}) %collective-permute-start.12) | collective-permute-done | bytes 1048608 | tf_op jit(solution)/shard_map/ppermute | solution.py:23
  440.3 20.8 %collective-permute-done.17 = f32[256,1024]{0,1:T(8,128)S(1)} collective-permute-done((f32[256,1024]{0,1:T(8,128)S(1)}, f32[256,1024]{0,1:T(8,128)S(1)}, u32[]{:S(2)}, u32[]{:S(2)}) %collective-permute-start.17) | collective-permute-done | bytes 1048608 | tf_op jit(solution)/shard_map/ppermute | solution.py:23
  461.7 18.9 %collective-permute-done.13 = f32[256,1024]{0,1:T(8,128)S(1)} collective-permute-done((f32[256,1024]{0,1:T(8,128)S(1)}, f32[256,1024]{0,1:T(8,128)S(1)}, u32[]{:S(2)}, u32[]{:S(2)}) %collective-permute-start.13) | collective-permute-done | bytes 1048608 | tf_op jit(solution)/shard_map/ppermute | solution.py:23
  484.5 3.3 copy.49
  487.8 2.6 reshape.348
  490.4 3.3 collective-permute-done.8
  493.7 131.4 %all-reduce.3.cloned.1.call-done = (f32[5376,2,4,16]{0,3,2,1:T(8,128)}, f32[2,4,16,1024]{3,2,1,0:T(8,128)}) async-done(((f32[5376,2,4,16]{0,3,2,1:T(8,128)}, f32[2,4,16,1024]{3,2,1,0:T(8,128)}), (f32[5376,2,4,16]{0,3,2,1:T(8,128)}, f32[2,4,16,1024]{3,2,1,0:T(8,128)})) %all-reduce.3.cloned.1.call-update) | async-done | bytes 3276816 | tf_op jit(solution)/shard_map/psum | solution.py:285
  625.2 2.3 copy.113
  627.5 3.6 copy.114
  (303 shorter events, 127.7 us)
Async XLA Ops:
  7.2 618.0 %all-reduce.3.cloned.1.call-start = ((), (), s32[]{:S(2)}) async-start(), calls=%async_computation | async-start | bytes 6553600 | tf_op jit(solution)/shard_map/psum | solution.py:285
  7.2 4.4 copy-start.15
  15.5 8.0 %copy-start.5 = (bf16[2,4,16,1024]{3,2,1,0:T(8,128)(2,1)S(1)}, bf16[2,4,16,1024]{3,2,1,0:T(8,128)(2,1)}, u32[]{:S(2)}) copy-start(bf16[2,4,16,1024]{3,2,1,0:T(8,128)(2,1)} %param.21) | copy-start | bytes 786436
  15.5 8.0 %copy-start.22 = (bf16[1,256,1024]{2,1,0:T(8,128)(2,1)S(1)}, bf16[1,256,1024]{2,1,0:T(8,128)(2,1)}, u32[]{:S(2)}) copy-start(bf16[1,256,1024]{2,1,0:T(8,128)(2,1)} %param.16) | copy-start | bytes 1572868
  17.9 17.2 %collective-permute-start = (bf16[256,1024]{0,1:T(8,128)(2,1)S(1)}, bf16[256,1024]{0,1:T(8,128)(2,1)}, u32[]{:S(2)}, u32[]{:S(2)}) collective-permute-start(bf16[256,1024]{0,1:T(8,128)(2,1)S(1)} %bitcast.243), channel_id=1, source_target_pairs={{0,2},{2,4},{4,6},{6,8},{8,10},{10,12},{12,14},{1,3},{3,5},{5,7},{... | collective-permute-start | bytes 1572872 | tf_op jit(solution)/shard_map/ppermute | solution.py:23
  24.7 21.7 %collective-permute-start.4 = (bf16[256,1024]{1,0:T(8,128)(2,1)}, bf16[256,1024]{1,0:T(8,128)(2,1)}, u32[]{:S(2)}, u32[]{:S(2)}) collective-permute-start(bf16[256,1024]{1,0:T(8,128)(2,1)} %fusion.59), channel_id=1, source_target_pairs={{0,2},{2,4},{4,6},{6,8},{8,10},{10,12},{12,14},{1,3},{3,5},{5,7},{... | collective-permute-start | bytes 1572872 | tf_op jit(solution)/shard_map/ppermute | solution.py:23
  35.0 22.6 %collective-permute-start.1 = (bf16[256,1024]{0,1:T(8,128)(2,1)}, bf16[256,1024]{0,1:T(8,128)(2,1)}, u32[]{:S(2)}, u32[]{:S(2)}) collective-permute-start(bf16[256,1024]{0,1:T(8,128)(2,1)} %collective-permute-done), channel_id=1, source_target_pairs={{0,2},{2,4},{4,6},{6,8},{8,10},{10,12},{12,14},{1,3},{3,5},{5,7},{... | collective-permute-start | bytes 1572872 | tf_op jit(solution)/shard_map/ppermute | solution.py:23
  42.6 125.1 %collective-permute-start.9 = (bf16[1,256,2048]{1,2,0:T(8,128)(2,1)}, bf16[1,256,2048]{1,2,0:T(8,128)(2,1)}, u32[]{:S(2)}, u32[]{:S(2)}) collective-permute-start(bf16[1,256,2048]{1,2,0:T(8,128)(2,1)} %copy.50), channel_id=1, source_target_pairs={{0,16},{16,0},{1,17},{17,1},{2,18},{18,2},{3,19},{19,3},{4,20},{20... | collective-permute-start | bytes 3145736 | tf_op jit(solution)/shard_map/ppermute | solution.py:17
  46.4 22.5 %collective-permute-start.5 = (bf16[256,1024]{1,0:T(8,128)(2,1)}, bf16[256,1024]{1,0:T(8,128)(2,1)}, u32[]{:S(2)}, u32[]{:S(2)}) collective-permute-start(bf16[256,1024]{1,0:T(8,128)(2,1)} %collective-permute-done.4), channel_id=1, source_target_pairs={{0,2},{2,4},{4,6},{6,8},{8,10},{10,12},{12,14},{1,3},{3,5},{5,7},{... | collective-permute-start | bytes 1572872 | tf_op jit(solution)/shard_map/ppermute | solution.py:23
  57.6 22.5 %collective-permute-start.2 = (bf16[256,1024]{0,1:T(8,128)(2,1)}, bf16[256,1024]{0,1:T(8,128)(2,1)}, u32[]{:S(2)}, u32[]{:S(2)}) collective-permute-start(bf16[256,1024]{0,1:T(8,128)(2,1)} %collective-permute-done.1), channel_id=1, source_target_pairs={{0,2},{2,4},{4,6},{6,8},{8,10},{10,12},{12,14},{1,3},{3,5},{5,7},{... | collective-permute-start | bytes 1572872 | tf_op jit(solution)/shard_map/ppermute | solution.py:23
  66.9 17.6 %copy-start.1 = (f32[256,64]{1,0:T(8,128)S(1)}, f32[256,64]{1,0:T(8,128)}, u32[]{:S(2)}) copy-start(f32[256,64]{1,0:T(8,128)} %copy.41) | copy-start | bytes 196612
  66.9 17.6 %copy-start.2 = (f32[256,64]{1,0:T(8,128)S(1)}, f32[256,64]{1,0:T(8,128)}, u32[]{:S(2)}) copy-start(f32[256,64]{1,0:T(8,128)} %copy.43) | copy-start | bytes 196612
  68.8 22.5 %collective-permute-start.6 = (bf16[256,1024]{1,0:T(8,128)(2,1)}, bf16[256,1024]{1,0:T(8,128)(2,1)}, u32[]{:S(2)}, u32[]{:S(2)}) collective-permute-start(bf16[256,1024]{1,0:T(8,128)(2,1)} %collective-permute-done.5), channel_id=1, source_target_pairs={{0,2},{2,4},{4,6},{6,8},{8,10},{10,12},{12,14},{1,3},{3,5},{5,7},{... | collective-permute-start | bytes 1572872 | tf_op jit(solution)/shard_map/ppermute | solution.py:23
  80.1 22.5 %collective-permute-start.3 = (bf16[256,1024]{0,1:T(8,128)(2,1)}, bf16[256,1024]{0,1:T(8,128)(2,1)S(1)}, u32[]{:S(2)}, u32[]{:S(2)}) collective-permute-start(bf16[256,1024]{0,1:T(8,128)(2,1)} %collective-permute-done.2), channel_id=1, source_target_pairs={{0,2},{2,4},{4,6},{6,8},{8,10},{10,12},{12,14},{1,3},{3,5},{5,7},{... | collective-permute-start | bytes 1572872 | tf_op jit(solution)/shard_map/ppermute | solution.py:23
  91.3 22.9 %collective-permute-start.7 = (bf16[256,1024]{1,0:T(8,128)(2,1)}, bf16[256,1024]{1,0:T(8,128)(2,1)}, u32[]{:S(2)}, u32[]{:S(2)}) collective-permute-start(bf16[256,1024]{1,0:T(8,128)(2,1)} %collective-permute-done.6), channel_id=1, source_target_pairs={{0,2},{2,4},{4,6},{6,8},{8,10},{10,12},{12,14},{1,3},{3,5},{5,7},{... | collective-permute-start | bytes 1572872 | tf_op jit(solution)/shard_map/ppermute | solution.py:23
  167.7 4.5 copy-start.9
  167.7 4.5 copy-start.13
  167.7 4.5 copy-start.17
  183.5 4.6 copy-start.9
  183.5 4.6 copy-start.13
  183.5 4.6 copy-start.17
  199.4 4.6 copy-start.9
  199.4 4.6 copy-start.13
  199.4 4.5 copy-start.17
  212.2 3.1 copy-start.10
  212.2 3.1 copy-start.14
  212.2 3.1 copy-start.18
  215.3 4.6 copy-start.9
  215.3 4.6 copy-start.13
  215.3 4.6 copy-start.17
  228.1 3.1 copy-start.10
  228.1 3.1 copy-start.14
  228.1 3.1 copy-start.18
  231.2 4.6 copy-start.9
  231.3 4.6 copy-start.13
  231.3 4.6 copy-start.17
  244.1 3.0 copy-start.14
  244.1 3.0 copy-start.18
  247.1 4.6 copy-start.9
  247.1 4.5 copy-start.13
  247.1 4.5 copy-start.17
  259.9 3.0 copy-start.10
  259.9 3.0 copy-start.14
  259.9 3.1 copy-start.18
  263.0 4.6 copy-start.9
  263.0 4.6 copy-start.13
  263.0 4.6 copy-start.17
  278.9 4.6 copy-start.9
  278.9 4.6 copy-start.13
  278.9 4.5 copy-start.17
  294.7 4.5 slice-start
  294.7 4.5 slice-start.1
  297.8 28.4 %collective-permute-start.14 = (f32[256,1024]{0,1:T(8,128)S(1)}, f32[256,1024]{0,1:T(8,128)S(1)}, u32[]{:S(2)}, u32[]{:S(2)}) collective-permute-start(f32[256,1024]{0,1:T(8,128)S(1)} %bitcast.238), channel_id=1, source_target_pairs={{2,0},{4,2},{6,4},{8,6},{10,8},{12,10},{14,12},{3,1},{5,3},{7,5},{... | collective-permute-start | bytes 3145736 | tf_op jit(solution)/shard_map/ppermute | solution.py:23
  299.9 48.7 %collective-permute-start.10 = (f32[256,1024]{0,1:T(8,128)S(1)}, f32[256,1024]{0,1:T(8,128)S(1)}, u32[]{:S(2)}, u32[]{:S(2)}) collective-permute-start(f32[256,1024]{0,1:T(8,128)S(1)} %bitcast.239), channel_id=1, source_target_pairs={{2,0},{4,2},{6,4},{8,6},{10,8},{12,10},{14,12},{3,1},{5,3},{7,5},{... | collective-permute-start | bytes 3145736 | tf_op jit(solution)/shard_map/ppermute | solution.py:23
  326.3 44.8 %collective-permute-start.15 = (f32[256,1024]{0,1:T(8,128)S(1)}, f32[256,1024]{0,1:T(8,128)S(1)}, u32[]{:S(2)}, u32[]{:S(2)}) collective-permute-start(f32[256,1024]{0,1:T(8,128)S(1)} %bitcast_add_fusion.3), channel_id=1, source_target_pairs={{2,0},{4,2},{6,4},{8,6},{10,8},{12,10},{14,12},{3,1},{5,3},{7,5},{... | collective-permute-start | bytes 3145736 | tf_op jit(solution)/shard_map/ppermute | solution.py:23
  348.8 44.8 %collective-permute-start.11 = (f32[256,1024]{0,1:T(8,128)S(1)}, f32[256,1024]{0,1:T(8,128)S(1)}, u32[]{:S(2)}, u32[]{:S(2)}) collective-permute-start(f32[256,1024]{0,1:T(8,128)S(1)} %bitcast_add_fusion.7), channel_id=1, source_target_pairs={{2,0},{4,2},{6,4},{8,6},{10,8},{12,10},{14,12},{3,1},{5,3},{7,5},{... | collective-permute-start | bytes 3145736 | tf_op jit(solution)/shard_map/ppermute | solution.py:23
  371.3 44.8 %collective-permute-start.16 = (f32[256,1024]{0,1:T(8,128)S(1)}, f32[256,1024]{0,1:T(8,128)S(1)}, u32[]{:S(2)}, u32[]{:S(2)}) collective-permute-start(f32[256,1024]{0,1:T(8,128)S(1)} %bitcast_add_fusion.2), channel_id=1, source_target_pairs={{2,0},{4,2},{6,4},{8,6},{10,8},{12,10},{14,12},{3,1},{5,3},{7,5},{... | collective-permute-start | bytes 3145736 | tf_op jit(solution)/shard_map/ppermute | solution.py:23
  393.7 44.8 %collective-permute-start.12 = (f32[256,1024]{0,1:T(8,128)S(1)}, f32[256,1024]{0,1:T(8,128)S(1)}, u32[]{:S(2)}, u32[]{:S(2)}) collective-permute-start(f32[256,1024]{0,1:T(8,128)S(1)} %bitcast_add_fusion.6), channel_id=1, source_target_pairs={{2,0},{4,2},{6,4},{8,6},{10,8},{12,10},{14,12},{3,1},{5,3},{7,5},{... | collective-permute-start | bytes 3145736 | tf_op jit(solution)/shard_map/ppermute | solution.py:23
  416.1 24.1 %copy-start.6 = (bf16[2,4,16,1024]{3,2,1,0:T(8,128)(2,1)S(1)}, bf16[2,4,16,1024]{3,2,1,0:T(8,128)(2,1)}, u32[]{:S(2)}) copy-start(bf16[2,4,16,1024]{3,2,1,0:T(8,128)(2,1)} %param.21) | copy-start | bytes 786436
  416.2 44.8 %collective-permute-start.17 = (f32[256,1024]{0,1:T(8,128)S(1)}, f32[256,1024]{0,1:T(8,128)S(1)}, u32[]{:S(2)}, u32[]{:S(2)}) collective-permute-start(f32[256,1024]{0,1:T(8,128)S(1)} %bitcast_add_fusion.1), channel_id=1, source_target_pairs={{2,0},{4,2},{6,4},{8,6},{10,8},{12,10},{14,12},{3,1},{5,3},{7,5},{... | collective-permute-start | bytes 3145736 | tf_op jit(solution)/shard_map/ppermute | solution.py:23
  438.7 42.0 %collective-permute-start.13 = (f32[256,1024]{0,1:T(8,128)S(1)}, f32[256,1024]{0,1:T(8,128)S(1)}, u32[]{:S(2)}, u32[]{:S(2)}) collective-permute-start(f32[256,1024]{0,1:T(8,128)S(1)} %bitcast_add_fusion.5), channel_id=1, source_target_pairs={{2,0},{4,2},{6,4},{8,6},{10,8},{12,10},{14,12},{3,1},{5,3},{7,5},{... | collective-permute-start | bytes 3145736 | tf_op jit(solution)/shard_map/ppermute | solution.py:23
  461.2 19.6 %copy-start.7 = (f32[256,64]{0,1:T(8,128)S(1)}, f32[256,64]{0,1:T(8,128)}, u32[]{:S(2)}) copy-start(f32[256,64]{0,1:T(8,128)} %get-tuple-element.290) | copy-start | bytes 196612
  490.4 3.3 collective-permute-start.8
  627.5 3.6 copy-start.3
  (22 other events, 56.3 us)
Sparse Core Ops, SparseCore 0:
  484.6 140.5 all-reduce.2
where the time goes:
time: 642 us; the launch traced here: 639 us
  waiting for transfers between devices  336 us (52%)
  matrix products  123 us (19%)
  local copies, waits for them, and re-layouts  75.9 us (12%)
  starting transfers between devices  50.3 us (8%)
  other arithmetic  39.1 us (6%)
  between operations  14.5 us (2%)
    ppermute x16, waiting for transfers between devices, passed_along_2(): lax.ppermute(value, axis, [(source, source + steps) for source in range(i...  201 us
    psum x1, waiting for transfers between devices, body(): lax.psum((down_map_gradient, up_map_gradient), ('section', 'ctx', 'dp'))  131 us
    ppermute x16, starting transfers between devices, passed_along_2(): lax.ppermute(value, axis, [(source, source + steps) for source in range(i...  50.3 us
    dot_general x16, matrix products, masked_scores(): jnp.einsum('trd,ld->trl', query_part, key_part, preferred_element_type=jn...  40.9 us
    dot_general x8, matrix products, group_backward(): jnp.einsum('trl,trd->ld', grad_scores, query_part, preferred_element_type...  31.1 us
    unnamed x52, local copies, waits for them, and re-layouts  26.1 us
    dot_general x8, matrix products, group_backward(): jnp.einsum('trl,trd->ld', weights_low, grad_part, preferred_element_type=...  24.3 us
    dot_general x8, matrix products, group_forward(): jnp.einsum('trl,ld->trd', weights, value_part, preferred_element_type=jnp...  18.2 us
  transfers between devices with their start and end apart: 19, of which 17 were waited for; matrix products, arithmetic and copies ran while one was open for 14% of the time, Pallas kernels for 0%

commit v1 on v0

--- a/solution.py
+++ b/solution.py
@@ -3,6 +3,7 @@
 import jax.numpy as jnp
 from jax import lax
 from jax.sharding import PartitionSpec as P
+from jax.lax import psum
 
 HD = 128
 WINDOW = 1024
@@ -10,6 +11,12 @@
 adapter_scale = 0.5
 rope_base = 10000.0
 masked_score = -1e30
+
+
+def follow_the_weights(my_data, shard_axis, mesh_name):
+    for rr in (shard_axis, mesh_name):
+        my_data = psum(my_data, rr)
+    return my_data
 
 
 def passed_along(value, axis, by):
@@ -282,7 +289,7 @@
         value_gradient,
         adapter_up_maps,
     )
-    summed = lax.psum((down_map_gradient, up_map_gradient), ("section", "ctx", "dp"))
+    summed = follow_the_weights((down_map_gradient, up_map_gradient), "section", ("ctx", "dp"))
     return (handed, summed[0], summed[1])
 
 

time: 642 us -> 683 us (1.064)
  waiting for transfers between devices: 336 us -> 377 us
    psum x1 -> x2, waiting for transfers between devices: 131 us -> 173 us  [follow_the_weights(): my_data = psum(my_data, rr)]
  transfers between devices with their start and end apart: 19 -> 20, of which waited for: 17 -> 18; matrix products, arithmetic and copies ran while one was open for 14% -> 13% of each run, Pallas kernels for 0% -> 0%
where the time goes in v1:
time: 683 us; the launch traced here: 680 us
  waiting for transfers between devices  377 us (55%)
  matrix products  122 us (18%)
  local copies, waits for them, and re-layouts  75.9 us (11%)
  starting transfers between devices  50.4 us (7%)
  other arithmetic  39.1 us (6%)
  between operations  14.6 us (2%)
    ppermute x16, waiting for transfers between devices, passed_along_2(): lax.ppermute(value, axis, [(source, source + steps) for source in range(i...  201 us
    psum x2, waiting for transfers between devices, follow_the_weights(): my_data = psum(my_data, rr)  173 us
    ppermute x16, starting transfers between devices, passed_along_2(): lax.ppermute(value, axis, [(source, source + steps) for source in range(i...  50.1 us
    dot_general x16, matrix products, masked_scores(): jnp.einsum('trd,ld->trl', query_part, key_part, preferred_element_type=jn...  41 us
    dot_general x8, matrix products, group_backward(): jnp.einsum('trl,trd->ld', grad_scores, query_part, preferred_element_type...  31 us
    unnamed x52, local copies, waits for them, and re-layouts  26.1 us
    dot_general x8, matrix products, group_backward(): jnp.einsum('trl,trd->ld', weights_low, grad_part, preferred_element_type=...  24.3 us
    dot_general x8, matrix products, group_forward(): jnp.einsum('trl,ld->trd', weights, value_part, preferred_element_type=jnp...  18.2 us
  transfers between devices with their start and end apart: 20, of which 18 were waited for; matrix products, arithmetic and copies ran while one was open for 13% of the time, Pallas kernels for 0%

profile of v1, /device:TPU:0, one launch (start us, length us, event | category | flops | bytes accessed | tf_op | source)
XLA Modules:
  0.0 680.0 jit_solution(1407792490667414575)
XLA Ops:
  9.2 2.4 fusion.65
  13.0 2.5 copy.58
  17.8 5.7 collective-permute-start
  24.7 3.5 collective-permute-start.4
  28.1 6.9 %collective-permute-done = bf16[256,1024]{0,1:T(8,128)(2,1)} collective-permute-done((bf16[256,1024]{0,1:T(8,128)(2,1)S(1)}, bf16[256,1024]{0,1:T(8,128)(2,1)}, u32[]{:S(2)}, u32[]{:S(2)}) %collective-permute-start) | collective-permute-done | bytes 524320 | tf_op jit(solution)/shard_map/ppermute | solution.py:30
  35.0 5.3 collective-permute-start.1
  42.6 2.8 convert_bitcast_fusion
  46.4 5.2 collective-permute-start.5
  51.6 6.0 collective-permute-done.1
  57.6 5.2 collective-permute-start.2
  68.8 5.2 collective-permute-start.6
  74.1 6.0 collective-permute-done.2
  80.1 4.4 collective-permute-start.3
  87.5 3.9 collective-permute-done.6
  91.3 5.2 collective-permute-start.7
  96.5 6.1 collective-permute-done.3
  109.8 4.4 copy.48
  121.6 46.0 %while.26 = (s32[]{:T(128)}, bf16[8,256,2,128]{3,1,2,0:T(8,128)(2,1)}, f32[8,256,2]{1,2,0:T(2,128)}, bf16[8,256,2,128]{3,1,2,0:T(8,128)(2,1)}, bf16[8,1280,128]{...) while((s32[]{:T(128)}, ...), condition=%wide.region_8.9_spmd.clone, body=%wide.region_5.8_spmd.clone.sunk | while | flops 343145984 | bytes 9469813 | solution.py:252
  136.6 2.3 fusion.119
  142.4 2.3 fusion.119
  148.1 2.3 fusion.119
  159.6 2.3 fusion.119
  165.4 2.3 fusion.119
  167.6 127.1 %while.27 = (s32[]{:T(128)}, f32[8,1280,128]{1,2,0:T(8,128)}, f32[8,1280,128]{1,2,0:T(8,128)}, bf16[8,256,2,128]{3,1,2,0:T(8,128)(2,1)}, bf16[8,1280,128]{2,1,0:...) while((s32[]{:T(128)}, f32[8,1280,128]{1,2,0:T(8,128)}, ...), condition=%wide.region_11.12_spmd.clone, body=%wide.region_9.11_spmd.clone.sunk | while | flops 678395392 | bytes 14472769 | solution.py:258
  168.9 3.3 fusion.128
  174.4 3.9 fusion.130
  180.5 3.0 fusion.131
  184.7 3.3 fusion.128
  190.2 3.9 fusion.130
  196.3 3.0 fusion.131
  200.7 3.3 fusion.128
  206.1 3.9 fusion.130
  212.2 3.1 fusion.131
  216.5 3.3 fusion.128
  222.0 3.9 fusion.130
  228.1 3.1 fusion.131
  232.5 3.3 fusion.128
  237.9 3.9 fusion.130
  244.0 3.0 fusion.131
  248.3 3.3 fusion.128
  253.8 3.9 fusion.130
  259.9 3.0 fusion.131
  264.2 3.3 fusion.128
  269.6 3.9 fusion.130
  275.8 3.0 fusion.131
  280.1 3.3 fusion.128
  285.6 3.9 fusion.130
  291.7 3.0 fusion.131
  294.7 3.0 fusion.84
  301.3 24.9 %collective-permute-done.14 = f32[256,1024]{0,1:T(8,128)S(1)} collective-permute-done((f32[256,1024]{0,1:T(8,128)S(1)}, f32[256,1024]{0,1:T(8,128)S(1)}, u32[]{:S(2)}, u32[]{:S(2)}) %collective-permute-start.14) | collective-permute-done | bytes 1048608 | tf_op jit(solution)/shard_map/ppermute | solution.py:30
  327.6 21.0 %collective-permute-done.10 = f32[256,1024]{0,1:T(8,128)S(1)} collective-permute-done((f32[256,1024]{0,1:T(8,128)S(1)}, f32[256,1024]{0,1:T(8,128)S(1)}, u32[]{:S(2)}, u32[]{:S(2)}) %collective-permute-start.10) | collective-permute-done | bytes 1048608 | tf_op jit(solution)/shard_map/ppermute | solution.py:30
  350.1 21.0 %collective-permute-done.15 = f32[256,1024]{0,1:T(8,128)S(1)} collective-permute-done((f32[256,1024]{0,1:T(8,128)S(1)}, f32[256,1024]{0,1:T(8,128)S(1)}, u32[]{:S(2)}, u32[]{:S(2)}) %collective-permute-start.15) | collective-permute-done | bytes 1048608 | tf_op jit(solution)/shard_map/ppermute | solution.py:30
  372.6 21.0 %collective-permute-done.11 = f32[256,1024]{0,1:T(8,128)S(1)} collective-permute-done((f32[256,1024]{0,1:T(8,128)S(1)}, f32[256,1024]{0,1:T(8,128)S(1)}, u32[]{:S(2)}, u32[]{:S(2)}) %collective-permute-start.11) | collective-permute-done | bytes 1048608 | tf_op jit(solution)/shard_map/ppermute | solution.py:30
  395.0 21.0 %collective-permute-done.16 = f32[256,1024]{0,1:T(8,128)S(1)} collective-permute-done((f32[256,1024]{0,1:T(8,128)S(1)}, f32[256,1024]{0,1:T(8,128)S(1)}, u32[]{:S(2)}, u32[]{:S(2)}) %collective-permute-start.16) | collective-permute-done | bytes 1048608 | tf_op jit(solution)/shard_map/ppermute | solution.py:30
  417.5 21.0 %collective-permute-done.12 = f32[256,1024]{0,1:T(8,128)S(1)} collective-permute-done((f32[256,1024]{0,1:T(8,128)S(1)}, f32[256,1024]{0,1:T(8,128)S(1)}, u32[]{:S(2)}, u32[]{:S(2)}) %collective-permute-start.12) | collective-permute-done | bytes 1048608 | tf_op jit(solution)/shard_map/ppermute | solution.py:30
  440.0 21.0 %collective-permute-done.17 = f32[256,1024]{0,1:T(8,128)S(1)} collective-permute-done((f32[256,1024]{0,1:T(8,128)S(1)}, f32[256,1024]{0,1:T(8,128)S(1)}, u32[]{:S(2)}, u32[]{:S(2)}) %collective-permute-start.17) | collective-permute-done | bytes 1048608 | tf_op jit(solution)/shard_map/ppermute | solution.py:30
  461.7 18.9 %collective-permute-done.13 = f32[256,1024]{0,1:T(8,128)S(1)} collective-permute-done((f32[256,1024]{0,1:T(8,128)S(1)}, f32[256,1024]{0,1:T(8,128)S(1)}, u32[]{:S(2)}, u32[]{:S(2)}) %collective-permute-start.13) | collective-permute-done | bytes 1048608 | tf_op jit(solution)/shard_map/ppermute | solution.py:30
  484.6 25.2 %all-reduce.7.cloned.1.call-done = (f32[5376,2,4,16]{0,3,2,1:T(8,128)}, f32[2,4,16,1024]{3,2,1,0:T(8,128)}) async-done(((f32[5376,2,4,16]{0,3,2,1:T(8,128)}, f32[2,4,16,1024]{3,2,1,0:T(8,128)}), (f32[5376,2,4,16]{0,3,2,1:T(8,128)}, f32[2,4,16,1024]{3,2,1,0:T(8,128)})) %all-reduce.7.cloned.1.call-update) | async-done | bytes 3276816 | tf_op jit(solution)/shard_map/psum | solution.py:18
  509.8 3.3 copy.49
  513.1 2.6 reshape.348
  515.9 2.8 collective-permute-done.8
  518.7 147.8 %all-reduce.5.cloned.1.call-done = (f32[5376,2,4,16]{0,3,2,1:T(8,128)}, f32[2,4,16,1024]{3,2,1,0:T(8,128)}) async-done(((f32[5376,2,4,16]{0,3,2,1:T(8,128)}, f32[2,4,16,1024]{3,2,1,0:T(8,128)}), (f32[5376,2,4,16]{0,3,2,1:T(8,128)}, f32[2,4,16,1024]{3,2,1,0:T(8,128)})) %all-reduce.5.cloned.1.call-update) | async-done | bytes 3276816 | tf_op jit(solution)/shard_map/psum | solution.py:18
  666.5 2.3 copy.115
  668.8 3.6 copy.116
  (306 shorter events, 130.1 us)
Async XLA Ops:
  7.2 502.6 %all-reduce.7.cloned.1.call-start = ((), (), s32[]{:S(2)}) async-start(), calls=%async_computation.1 | async-start | bytes 6553600 | tf_op jit(solution)/shard_map/psum | solution.py:18
  7.2 4.4 copy-start.15
  15.5 8.0 %copy-start.5 = (bf16[2,4,16,1024]{3,2,1,0:T(8,128)(2,1)S(1)}, bf16[2,4,16,1024]{3,2,1,0:T(8,128)(2,1)}, u32[]{:S(2)}) copy-start(bf16[2,4,16,1024]{3,2,1,0:T(8,128)(2,1)} %param.21) | copy-start | bytes 786436
  15.5 8.0 %copy-start.22 = (bf16[1,256,1024]{2,1,0:T(8,128)(2,1)S(1)}, bf16[1,256,1024]{2,1,0:T(8,128)(2,1)}, u32[]{:S(2)}) copy-start(bf16[1,256,1024]{2,1,0:T(8,128)(2,1)} %param.16) | copy-start | bytes 1572868
  17.8 17.2 %collective-permute-start = (bf16[256,1024]{0,1:T(8,128)(2,1)S(1)}, bf16[256,1024]{0,1:T(8,128)(2,1)}, u32[]{:S(2)}, u32[]{:S(2)}) collective-permute-start(bf16[256,1024]{0,1:T(8,128)(2,1)S(1)} %bitcast.243), channel_id=1, source_target_pairs={{0,2},{2,4},{4,6},{6,8},{8,10},{10,12},{12,14},{1,3},{3,5},{5,7},{... | collective-permute-start | bytes 1572872 | tf_op jit(solution)/shard_map/ppermute | solution.py:30
  24.7 21.7 %collective-permute-start.4 = (bf16[256,1024]{1,0:T(8,128)(2,1)}, bf16[256,1024]{1,0:T(8,128)(2,1)}, u32[]{:S(2)}, u32[]{:S(2)}) collective-permute-start(bf16[256,1024]{1,0:T(8,128)(2,1)} %fusion.59), channel_id=1, source_target_pairs={{0,2},{2,4},{4,6},{6,8},{8,10},{10,12},{12,14},{1,3},{3,5},{5,7},{... | collective-permute-start | bytes 1572872 | tf_op jit(solution)/shard_map/ppermute | solution.py:30
  35.0 22.6 %collective-permute-start.1 = (bf16[256,1024]{0,1:T(8,128)(2,1)}, bf16[256,1024]{0,1:T(8,128)(2,1)}, u32[]{:S(2)}, u32[]{:S(2)}) collective-permute-start(bf16[256,1024]{0,1:T(8,128)(2,1)} %collective-permute-done), channel_id=1, source_target_pairs={{0,2},{2,4},{4,6},{6,8},{8,10},{10,12},{12,14},{1,3},{3,5},{5,7},{... | collective-permute-start | bytes 1572872 | tf_op jit(solution)/shard_map/ppermute | solution.py:30
  42.6 125.1 %collective-permute-start.9 = (bf16[1,256,2048]{1,2,0:T(8,128)(2,1)}, bf16[1,256,2048]{1,2,0:T(8,128)(2,1)}, u32[]{:S(2)}, u32[]{:S(2)}) collective-permute-start(bf16[1,256,2048]{1,2,0:T(8,128)(2,1)} %copy.50), channel_id=1, source_target_pairs={{0,16},{16,0},{1,17},{17,1},{2,18},{18,2},{3,19},{19,3},{4,20},{20... | collective-permute-start | bytes 3145736 | tf_op jit(solution)/shard_map/ppermute | solution.py:24
  46.4 22.5 %collective-permute-start.5 = (bf16[256,1024]{1,0:T(8,128)(2,1)}, bf16[256,1024]{1,0:T(8,128)(2,1)}, u32[]{:S(2)}, u32[]{:S(2)}) collective-permute-start(bf16[256,1024]{1,0:T(8,128)(2,1)} %collective-permute-done.4), channel_id=1, source_target_pairs={{0,2},{2,4},{4,6},{6,8},{8,10},{10,12},{12,14},{1,3},{3,5},{5,7},{... | collective-permute-start | bytes 1572872 | tf_op jit(solution)/shard_map/ppermute | solution.py:30
  57.6 22.5 %collective-permute-start.2 = (bf16[256,1024]{0,1:T(8,128)(2,1)}, bf16[256,1024]{0,1:T(8,128)(2,1)}, u32[]{:S(2)}, u32[]{:S(2)}) collective-permute-start(bf16[256,1024]{0,1:T(8,128)(2,1)} %collective-permute-done.1), channel_id=1, source_target_pairs={{0,2},{2,4},{4,6},{6,8},{8,10},{10,12},{12,14},{1,3},{3,5},{5,7},{... | collective-permute-start | bytes 1572872 | tf_op jit(solution)/shard_map/ppermute | solution.py:30
  66.9 17.5 %copy-start.1 = (f32[256,64]{1,0:T(8,128)S(1)}, f32[256,64]{1,0:T(8,128)}, u32[]{:S(2)}) copy-start(f32[256,64]{1,0:T(8,128)} %copy.41) | copy-start | bytes 196612
  67.0 17.5 %copy-start.2 = (f32[256,64]{1,0:T(8,128)S(1)}, f32[256,64]{1,0:T(8,128)}, u32[]{:S(2)}) copy-start(f32[256,64]{1,0:T(8,128)} %copy.43) | copy-start | bytes 196612
  68.8 22.5 %collective-permute-start.6 = (bf16[256,1024]{1,0:T(8,128)(2,1)}, bf16[256,1024]{1,0:T(8,128)(2,1)}, u32[]{:S(2)}, u32[]{:S(2)}) collective-permute-start(bf16[256,1024]{1,0:T(8,128)(2,1)} %collective-permute-done.5), channel_id=1, source_target_pairs={{0,2},{2,4},{4,6},{6,8},{8,10},{10,12},{12,14},{1,3},{3,5},{5,7},{... | collective-permute-start | bytes 1572872 | tf_op jit(solution)/shard_map/ppermute | solution.py:30
  80.1 22.5 %collective-permute-start.3 = (bf16[256,1024]{0,1:T(8,128)(2,1)}, bf16[256,1024]{0,1:T(8,128)(2,1)S(1)}, u32[]{:S(2)}, u32[]{:S(2)}) collective-permute-start(bf16[256,1024]{0,1:T(8,128)(2,1)} %collective-permute-done.2), channel_id=1, source_target_pairs={{0,2},{2,4},{4,6},{6,8},{8,10},{10,12},{12,14},{1,3},{3,5},{5,7},{... | collective-permute-start | bytes 1572872 | tf_op jit(solution)/shard_map/ppermute | solution.py:30
  91.3 22.9 %collective-permute-start.7 = (bf16[256,1024]{1,0:T(8,128)(2,1)}, bf16[256,1024]{1,0:T(8,128)(2,1)}, u32[]{:S(2)}, u32[]{:S(2)}) collective-permute-start(bf16[256,1024]{1,0:T(8,128)(2,1)} %collective-permute-done.6), channel_id=1, source_target_pairs={{0,2},{2,4},{4,6},{6,8},{8,10},{10,12},{12,14},{1,3},{3,5},{5,7},{... | collective-permute-start | bytes 1572872 | tf_op jit(solution)/shard_map/ppermute | solution.py:30
  167.6 4.6 copy-start.9
  167.6 4.6 copy-start.13
  167.7 4.6 copy-start.17
  183.5 4.6 copy-start.9
  183.5 4.6 copy-start.13
  183.5 4.6 copy-start.17
  199.4 4.6 copy-start.9
  199.4 4.6 copy-start.13
  199.4 4.6 copy-start.17
  212.2 3.1 copy-start.10
  212.2 3.1 copy-start.14
  212.2 3.1 copy-start.18
  215.3 4.6 copy-start.9
  215.3 4.6 copy-start.13
  215.4 4.6 copy-start.17
  228.1 3.1 copy-start.10
  228.1 3.1 copy-start.14
  228.1 3.1 copy-start.18
  231.2 4.6 copy-start.9
  231.2 4.6 copy-start.13
  231.3 4.6 copy-start.17
  247.1 4.6 copy-start.9
  247.1 4.6 copy-start.13
  247.1 4.6 copy-start.17
  259.9 3.1 copy-start.10
  259.9 3.1 copy-start.14
  259.9 3.1 copy-start.18
  262.9 4.6 copy-start.9
  263.0 4.6 copy-start.13
  263.0 4.6 copy-start.17
  275.8 3.0 copy-start.18
  278.8 4.6 copy-start.9
  278.8 4.6 copy-start.13
  278.8 4.6 copy-start.17
  294.7 4.5 slice-start
  294.7 4.5 slice-start.1
  297.8 28.4 %collective-permute-start.14 = (f32[256,1024]{0,1:T(8,128)S(1)}, f32[256,1024]{0,1:T(8,128)S(1)}, u32[]{:S(2)}, u32[]{:S(2)}) collective-permute-start(f32[256,1024]{0,1:T(8,128)S(1)} %bitcast.238), channel_id=1, source_target_pairs={{2,0},{4,2},{6,4},{8,6},{10,8},{12,10},{14,12},{3,1},{5,3},{7,5},{... | collective-permute-start | bytes 3145736 | tf_op jit(solution)/shard_map/ppermute | solution.py:30
  300.0 48.7 %collective-permute-start.10 = (f32[256,1024]{0,1:T(8,128)S(1)}, f32[256,1024]{0,1:T(8,128)S(1)}, u32[]{:S(2)}, u32[]{:S(2)}) collective-permute-start(f32[256,1024]{0,1:T(8,128)S(1)} %bitcast.239), channel_id=1, source_target_pairs={{2,0},{4,2},{6,4},{8,6},{10,8},{12,10},{14,12},{3,1},{5,3},{7,5},{... | collective-permute-start | bytes 3145736 | tf_op jit(solution)/shard_map/ppermute | solution.py:30
  326.3 44.8 %collective-permute-start.15 = (f32[256,1024]{0,1:T(8,128)S(1)}, f32[256,1024]{0,1:T(8,128)S(1)}, u32[]{:S(2)}, u32[]{:S(2)}) collective-permute-start(f32[256,1024]{0,1:T(8,128)S(1)} %bitcast_add_fusion.3), channel_id=1, source_target_pairs={{2,0},{4,2},{6,4},{8,6},{10,8},{12,10},{14,12},{3,1},{5,3},{7,5},{... | collective-permute-start | bytes 3145736 | tf_op jit(solution)/shard_map/ppermute | solution.py:30
  348.8 44.8 %collective-permute-start.11 = (f32[256,1024]{0,1:T(8,128)S(1)}, f32[256,1024]{0,1:T(8,128)S(1)}, u32[]{:S(2)}, u32[]{:S(2)}) collective-permute-start(f32[256,1024]{0,1:T(8,128)S(1)} %bitcast_add_fusion.7), channel_id=1, source_target_pairs={{2,0},{4,2},{6,4},{8,6},{10,8},{12,10},{14,12},{3,1},{5,3},{7,5},{... | collective-permute-start | bytes 3145736 | tf_op jit(solution)/shard_map/ppermute | solution.py:30
  371.3 44.8 %collective-permute-start.16 = (f32[256,1024]{0,1:T(8,128)S(1)}, f32[256,1024]{0,1:T(8,128)S(1)}, u32[]{:S(2)}, u32[]{:S(2)}) collective-permute-start(f32[256,1024]{0,1:T(8,128)S(1)} %bitcast_add_fusion.2), channel_id=1, source_target_pairs={{2,0},{4,2},{6,4},{8,6},{10,8},{12,10},{14,12},{3,1},{5,3},{7,5},{... | collective-permute-start | bytes 3145736 | tf_op jit(solution)/shard_map/ppermute | solution.py:30
  393.7 44.8 %collective-permute-start.12 = (f32[256,1024]{0,1:T(8,128)S(1)}, f32[256,1024]{0,1:T(8,128)S(1)}, u32[]{:S(2)}, u32[]{:S(2)}) collective-permute-start(f32[256,1024]{0,1:T(8,128)S(1)} %bitcast_add_fusion.6), channel_id=1, source_target_pairs={{2,0},{4,2},{6,4},{8,6},{10,8},{12,10},{14,12},{3,1},{5,3},{7,5},{... | collective-permute-start | bytes 3145736 | tf_op jit(solution)/shard_map/ppermute | solution.py:30
  416.1 23.9 %copy-start.6 = (bf16[2,4,16,1024]{3,2,1,0:T(8,128)(2,1)S(1)}, bf16[2,4,16,1024]{3,2,1,0:T(8,128)(2,1)}, u32[]{:S(2)}) copy-start(bf16[2,4,16,1024]{3,2,1,0:T(8,128)(2,1)} %param.21) | copy-start | bytes 786436
  416.2 44.8 %collective-permute-start.17 = (f32[256,1024]{0,1:T(8,128)S(1)}, f32[256,1024]{0,1:T(8,128)S(1)}, u32[]{:S(2)}, u32[]{:S(2)}) collective-permute-start(f32[256,1024]{0,1:T(8,128)S(1)} %bitcast_add_fusion.1), channel_id=1, source_target_pairs={{2,0},{4,2},{6,4},{8,6},{10,8},{12,10},{14,12},{3,1},{5,3},{7,5},{... | collective-permute-start | bytes 3145736 | tf_op jit(solution)/shard_map/ppermute | solution.py:30
  438.7 42.0 %collective-permute-start.13 = (f32[256,1024]{0,1:T(8,128)S(1)}, f32[256,1024]{0,1:T(8,128)S(1)}, u32[]{:S(2)}, u32[]{:S(2)}) collective-permute-start(f32[256,1024]{0,1:T(8,128)S(1)} %bitcast_add_fusion.5), channel_id=1, source_target_pairs={{2,0},{4,2},{6,4},{8,6},{10,8},{12,10},{14,12},{3,1},{5,3},{7,5},{... | collective-permute-start | bytes 3145736 | tf_op jit(solution)/shard_map/ppermute | solution.py:30
  461.2 19.6 %copy-start.7 = (f32[256,64]{0,1:T(8,128)S(1)}, f32[256,64]{0,1:T(8,128)}, u32[]{:S(2)}) copy-start(f32[256,64]{0,1:T(8,128)} %get-tuple-element.292) | copy-start | bytes 196612
  484.5 182.0 %all-reduce.5.cloned.1.call-start = ((), (), s32[]{:S(2)}) async-start(), calls=%async_computation | async-start | bytes 6553600 | tf_op jit(solution)/shard_map/psum | solution.py:18
  515.7 3.0 collective-permute-start.8
  668.8 3.6 copy-start.3
  (23 other events, 59.3 us)
Sparse Core Ops, SparseCore 0:
  484.6 25.0 all-reduce.6
  515.4 151.0 all-reduce.4
